TPU v7x, 512 devices: a whole 4x4x16 slice. The times are simulated.
512 devices in a mesh: rows: 16 (over y, z_lo), cols: 32 (over z_hi, x, core).
Axes of the slice: x: 4, y: 4, z: 16 (z_hi: 4, z_lo: 4; z = z_hi * 4 + z_lo), core: 2. Of those that a mesh axis runs over, the one named last changes fastest.
Arguments:
- factor_u: float32 [16, 8192, 128], P('rows', 'cols'), may hold values from -2 to 2
- factor_v: float32 [32, 2048, 128], P('cols', 'rows'), may hold values from -2 to 2
- values: bfloat16 [16, 32, 32, 256, 256], P('rows', 'cols'), may hold values from -6 to 6
- mask_words: int32 [16, 32, 32, 16, 256], P('rows', 'cols'), may hold values from 0 to 65535, as said below
- tile_cols: int32 [16, 32, 32], P('rows', 'cols'), may hold values from 0 to 7
Outputs:
- new_u: float32 [16, 8192, 128], P('rows', 'cols')
- new_v: float32 [32, 2048, 128], P('cols', 'rows')
- loss: float32 [], replicated
Inputs may be any that keep to these rules, and one draw needn't show every extreme that they name: `mask_words`: bit b of word w of a slot marks the entry in row 16 w + b of the tile.
All inputs are finite; a program needn't handle non-finite values.
Results may differ from a plain program's by a relative error of at most 0.02.
Values may be sent and summed in bfloat16 or wider, within the bound.
A program may use at most 64 MiB of HBM per device.

v0:
```python
import jax
import jax.numpy as jnp
from jax import lax
from jax.sharding import Mesh
from jax.sharding import PartitionSpec as P

ROWS = ("rows_0", "rows_1")
COLS = ("cols_0", "cols_1", "cols_2")
ROWS_COLS = ("rows_0", "rows_1", "cols_0", "cols_1", "cols_2")
step_rate = 0.01
ridge_weight = 0.1


def from_everyone(array, axis):
    copies = jnp.broadcast_to(array, (lax.axis_size(axis), *array.shape))
    return lax.all_to_all(copies, axis, split_axis=0, concat_axis=0, tiled=True)


def laid_out(tiles, dim):
    tiles = jnp.moveaxis(tiles, 0, dim)
    dims = tiles.shape
    return tiles.reshape(*dims[:dim], dims[dim] * dims[dim + 1], *dims[dim + 2 :])


def gathered_copies(array, axis, dim):
    tiles = from_everyone(array, axis)
    return laid_out(tiles, dim)


def in_blocks(array, dim, count):
    dims = array.shape
    tiles = array.reshape(*dims[:dim], count, dims[dim] // count, *dims[dim + 1 :])
    return jnp.moveaxis(tiles, dim, 0)


def sum_by_chip(array, chips, core, dim):
    sizes = (lax.axis_size(chips), lax.axis_size(core))
    tiles = in_blocks(array, dim, sizes[0] * sizes[1])
    inside = tiles.shape[1:]
    tiles = tiles.reshape(*sizes, *inside).swapaxes(0, 1).reshape(-1, *inside)
    tiles = lax.psum_scatter(tiles, core, scatter_dimension=0, tiled=True)
    return lax.psum_scatter(tiles, chips, scatter_dimension=0, tiled=True)[0]


def summed_on_arrival(array, axis, dim):
    count = lax.axis_size(axis)
    tiles = lax.all_to_all(in_blocks(array, dim, count), axis, 0, 0, tiled=True)
    return jnp.sum(tiles.astype(jnp.float32), axis=0)


def by_axis(array, axes):
    for axis in axes:
        array = lax.psum(array, axis)
    return array


def decode(mask_bits):
    shifts = jnp.arange(16, dtype=jnp.int32)
    bit_values = jnp.bitwise_and(
        jnp.right_shift(mask_bits[:, :, None, :], shifts[None, None, :, None]), 1
    )
    return bit_values.reshape(
        mask_bits.shape[0], mask_bits.shape[1] * 16, mask_bits.shape[2]
    ).astype(jnp.float32)


def slot_terms(left_rows, tile_values, mask_bits, column_ids, right_tiles):
    observed = decode(mask_bits)
    right_rows = jnp.take(right_tiles, column_ids, axis=0)
    predicted = jnp.einsum(
        "sik,sjk->sij", left_rows, right_rows, preferred_element_type=jnp.float32
    )
    residual = observed * (predicted - tile_values.astype(jnp.float32))
    squares = 0.5 * jnp.sum(residual * residual)
    resid_low = residual.astype(jnp.bfloat16)
    grad_rows = jnp.einsum(
        "sij,sjk->sik", resid_low, right_rows, preferred_element_type=jnp.float32
    )
    first = grad_rows.reshape(-1, left_rows.shape[2])
    grad_cols = jnp.einsum("sij,sik->sjk", resid_low, left_rows, preferred_element_type=jnp.float32)
    selector = (
        column_ids[:, None] == jnp.arange(right_tiles.shape[0], dtype=jnp.int32)[None, :]
    ).astype(jnp.float32)
    col_sums = jnp.einsum(
        "sq,sx->qx",
        selector,
        grad_cols.reshape(grad_cols.shape[0], -1),
        precision=lax.Precision.HIGHEST,
        preferred_element_type=jnp.float32,
    )
    return (first, col_sums, squares)


def band_terms(left_tiles, tile_values, mask_bits, column_ids, right_tiles):
    tile_count = left_tiles.shape[0]
    row_parts = []
    col_total = jnp.zeros(
        (right_tiles.shape[0], right_tiles.shape[1] * right_tiles.shape[2]), jnp.float32
    )
    square_total = jnp.zeros((), jnp.float32)
    for block_start in range(0, tile_count, 8):
        block_len = min(8, tile_count - block_start)
        block_end = block_start + block_len
        first, col_sums, squares = slot_terms(
            left_tiles[block_start:block_end],
            tile_values[block_start:block_end],
            mask_bits[block_start:block_end],
            column_ids[block_start:block_end],
            right_tiles,
        )
        row_parts.append(first)
        col_total = col_total + col_sums
        square_total = square_total + squares
    return (jnp.concatenate(row_parts, axis=0), col_total, square_total)


def per_device(factor_u, factor_v, values, mask_words, tile_cols):
    owned_left = factor_u[0]
    owned_right = factor_v[0]
    tile_values = values[0, 0]
    mask_bits = mask_words[0, 0]
    column_ids = tile_cols[0, 0]
    tile_size = tile_values.shape[-1]
    factor_rank = owned_left.shape[-1]
    slot_count = tile_values.shape[0]
    v_band = gathered_copies(owned_right.astype(jnp.bfloat16), ROWS, 0)
    right_tiles = v_band.reshape(-1, tile_size, factor_rank)
    u_low = owned_left.astype(jnp.bfloat16)
    u_band = lax.all_gather(u_low, COLS, axis=0, tiled=True)
    first_rows, col_total, square_total = band_terms(
        u_band.reshape(-1, tile_size, factor_rank), tile_values, mask_bits, column_ids, right_tiles
    )
    grad_u = sum_by_chip(first_rows.astype(jnp.bfloat16), ("cols_0", "cols_1"), "cols_2", 0).astype(
        jnp.float32
    )
    grad_v = summed_on_arrival(col_total.reshape(-1, factor_rank).astype(jnp.bfloat16), ROWS, 0)
    local_sum = square_total + 0.5 * ridge_weight * (
        jnp.sum(owned_left * owned_left) + jnp.sum(owned_right * owned_right)
    )
    total = by_axis(local_sum, ROWS_COLS)
    entries = lax.axis_size(ROWS) * lax.axis_size(COLS) * slot_count * tile_size * tile_size
    new_left = owned_left - step_rate * (grad_u + ridge_weight * owned_left)
    new_right = owned_right - step_rate * (grad_v + ridge_weight * owned_right)
    return (new_left[None], new_right[None], total / entries)


def solution(mesh):
    split = Mesh(
        mesh.devices.reshape(4, 4, 4, 4, 2), ("rows_0", "rows_1", "cols_0", "cols_1", "cols_2")
    )
    in_specs = (
        P(ROWS, COLS, None),
        P(COLS, ROWS, None),
        P(ROWS, COLS, None, None, None),
        P(ROWS, COLS, None, None, None),
        P(ROWS, COLS, None),
    )
    out_specs = (P(ROWS, COLS, None), P(COLS, ROWS, None), P())
    return jax.shard_map(
        per_device, mesh=split, in_specs=in_specs, out_specs=out_specs, check_vma=False
    )
```

profile of v0, /device:TPU:8, one launch (start us, length us, event | category | flops | bytes accessed | tf_op | source)
XLA Modules:
  0.0 256.3 jit_solution(2091023990044940334)
XLA Ops:
  7.2 0.0 all-gather.3.cloned.1.call-start
  7.2 2.2 multiply_reduce_fusion.4
  9.5 1.5 multiply_reduce_fusion.5
  11.0 0.9 broadcast_in_dim.11
  11.9 9.2 %all-to-all-start = ((bf16[16,128,128]{2,1,0:T(8,128)(2,1)}), bf16[16,128,128]{2,1,0:T(8,128)(2,1)S(1)}, u32[]{:S(2)}, u32[]{:S(2)}) async-start(bf16[16,128,128]{2,1,0:T(8,128)(2,1)} %broadcast_in_dim.11), calls=%async_computation | async-start | bytes 1048576 | tf_op jit(solution)/shard_map/all_to_all | solution.py:16
  21.1 3.9 %fusion.36 = (bf16[1,1,8,256,256]{4,3,2,1,0:T(8,128)(2,1)}, bf16[1,1,8,256,256]{4,3,2,1,0:T(8,128)(2,1)}, bf16[1,1,8,256,256]{4,3,2,1,0:T(8,128)(2,1)}, bf16[1,1,8,256,256]{4,3,2,1,0:T(8,128)(2,1)S(1)}) fusion(bf16[1,1,32,256,256]{4,3,2,1,0:T(8,128)(2,1)} %param.9), kind=kLoop, calls=%fused_computation.94 | loop fusion | bytes 8388608 | tf_op jit(solution)/shard_map/slice | solution.py:106
  25.0 1.3 copy.41
  26.4 1.5 shift_right_arithmetic.104
  27.9 1.9 copy.30
  29.8 0.1 shift_right_arithmetic.92
  29.9 2.2 copy.40
  32.2 1.6 shift_right_arithmetic.100
  33.7 2.9 %copy.27 = s32[8,256,256]{1,2,0:T(8,128)} copy(s32[8,256,256]{2,1,0:T(8,128)} %bitcast.116) | data formatting | bytes 4194304 | tf_op jit(solution)/shard_map/shift_right_arithmetic | solution.py:60
  36.7 2.3 copy.39
  38.9 1.5 shift_right_arithmetic.96
  40.4 2.9 %copy.24 = s32[8,256,256]{1,2,0:T(8,128)} copy(s32[8,256,256]{2,1,0:T(8,128)} %bitcast.117) | data formatting | bytes 4194304 | tf_op jit(solution)/shard_map/shift_right_arithmetic | solution.py:60
  43.3 2.3 copy.38
  45.6 1.5 shift_right_arithmetic.89
  47.1 2.9 %copy.21 = s32[8,256,256]{1,2,0:T(8,128)} copy(s32[8,256,256]{2,1,0:T(8,128)} %bitcast.118) | data formatting | bytes 4194304 | tf_op jit(solution)/shard_map/shift_right_arithmetic | solution.py:60
  50.0 0.1 compare_and_fusion.3
  50.1 1.4 gather_fusion.3
  51.5 1.4 gather_fusion.2
  52.9 1.4 gather_fusion.1
  54.3 1.4 gather_fusion
  55.8 38.8 %all-gather.3.cloned.1.call-done = bf16[1,8192,128]{2,1,0:T(8,128)(2,1)} async-done(((bf16[1,256,128]{2,1,0:T(8,128)(2,1)}), bf16[1,8192,128]{2,1,0:T(8,128)(2,1)}) %all-gather.3.cloned.1.call-update) | async-done | bytes 2097168 | tf_op jit(solution)/shard_map/all_gather | solution.py:129
  94.6 1.8 fusion.37
  96.4 0.8 copy-done.8
  97.2 1.5 multiply_reduce_fusion
  98.7 0.5 convolution_convert_fusion
  99.2 1.0 copy-done.3
  100.3 1.5 multiply_reduce_fusion.1
  101.7 0.5 convolution_convert_fusion.1
  102.3 1.0 copy-done.2
  103.3 1.5 multiply_reduce_fusion.2
  104.9 0.5 convolution_convert_fusion.2
  105.4 1.0 copy-done.1
  106.5 1.5 multiply_reduce_fusion.3
  108.0 1.0 copy-done
  109.0 0.5 convolution_convert_fusion.3
  109.5 0.1 pad_maximum_fusion
  109.6 1.6 copy.33
  111.2 0.1 slice_bitcast_fusion.4
  111.3 1.8 convolution_bitcast_fusion.3
  113.2 0.4 convolution_bitcast_fusion.2
  113.6 0.4 convolution_bitcast_fusion.1
  114.1 0.2 copy-done.9
  114.2 0.4 convolution_bitcast_fusion
  114.7 1.2 fusion.11
  115.9 1.2 convolution_add_fusion.2
  117.1 1.2 convolution_add_fusion.1
  118.4 1.3 fusion
  119.7 1.0 convert_element_type.106
  120.7 5.2 %all-to-all-start.1 = ((bf16[16,128,128]{2,1,0:T(8,128)(2,1)}), bf16[16,128,128]{2,1,0:T(8,128)(2,1)S(1)}, u32[]{:S(2)}, u32[]{:S(2)}) async-start(bf16[16,128,128]{2,1,0:T(8,128)(2,1)} %convert_element_type.106), calls=%async_computation.3 | async-start | bytes 1048576 | tf_op jit(solution)/shard_map/all_to_all | solution.py:47
  125.9 0.1 reduce-scatter.3.cloned.1.call-done
  126.0 0.6 reduce-scatter.5.cloned.1.call-update
  130.4 9.2 %psum.35 = f32[]{:T(128)} all-reduce(f32[]{:T(128)S(6)} %add.61), channel_id=1, replica_groups=mesh['rows_0'=4,'rows_1'=4,'cols_0'=4,'cols_1'=4,'cols_2'=2] {'rows_0'}, use_global_device_ids=true, to_apply=%region_9.11 | all-reduce | flops 1 | bytes 8 | tf_op jit(solution)/shard_map/psum | solution.py:53
  139.6 12.2 %psum.36 = f32[]{:T(128)} all-reduce(f32[]{:T(128)} %psum.35), channel_id=1, replica_groups=mesh['rows_0'=4,'rows_1'=4,'cols_0'=4,'cols_1'=4,'cols_2'=2] {'rows_1'}, use_global_device_ids=true, to_apply=%region_10.12 | all-reduce | flops 1 | bytes 8 | tf_op jit(solution)/shard_map/psum | solution.py:53
  151.8 16.5 %psum.37 = f32[]{:T(128)} all-reduce(f32[]{:T(128)} %psum.36), channel_id=1, replica_groups=mesh['rows_0'=4,'rows_1'=4,'cols_0'=4,'cols_1'=4,'cols_2'=2] {'cols_0'}, use_global_device_ids=true, to_apply=%region_11.13 | all-reduce | flops 1 | bytes 8 | tf_op jit(solution)/shard_map/psum | solution.py:53
  168.3 11.0 %psum.38 = f32[]{:T(128)} all-reduce(f32[]{:T(128)} %psum.37), channel_id=1, replica_groups=mesh['rows_0'=4,'rows_1'=4,'cols_0'=4,'cols_1'=4,'cols_2'=2] {'cols_1'}, use_global_device_ids=true, to_apply=%region_12.14 | all-reduce | flops 1 | bytes 8 | tf_op jit(solution)/shard_map/psum | solution.py:53
  179.3 3.1 %psum.39 = f32[]{:T(128)} all-reduce(f32[]{:T(128)} %psum.38), channel_id=1, replica_groups=mesh['rows_0'=4,'rows_1'=4,'cols_0'=4,'cols_1'=4,'cols_2'=2] {'cols_2'}, use_global_device_ids=true, to_apply=%region_13.15 | all-reduce | flops 1 | bytes 8 | tf_op jit(solution)/shard_map/psum | solution.py:53
  183.0 0.1 convert_reduce_fusion
  183.1 0.6 fusion.23
  183.8 63.4 %reduce-scatter.5.cloned.1.call-done = bf16[1,256,128]{2,1,0:T(8,128)(2,1)} async-done(((bf16[16,256,128]{2,1,0:T(8,128)(2,1)}), bf16[1,256,128]{2,1,0:T(8,128)(2,1)}) %reduce-scatter.5.cloned.1.call-update) | async-done | bytes 65552 | tf_op jit(solution)/shard_map/reduce_scatter | solution.py:42
  247.1 1.5 multiply_subtract_fusion
  (50 shorter events, 0.2 us)
Async XLA Ops:
  7.2 87.5 %all-gather.3.cloned.1.call-start = ((), (), s32[]{:S(2)}) async-start(), calls=%async_computation.6 | async-start | bytes 2162688 | tf_op jit(solution)/shard_map/all_gather | solution.py:129
  11.9 38.2 %all-to-all-start = ((bf16[16,128,128]{2,1,0:T(8,128)(2,1)}), bf16[16,128,128]{2,1,0:T(8,128)(2,1)S(1)}, u32[]{:S(2)}, u32[]{:S(2)}) async-start(bf16[16,128,128]{2,1,0:T(8,128)(2,1)} %broadcast_in_dim.11), calls=%async_computation | async-start | bytes 1048576 | tf_op jit(solution)/shard_map/all_to_all | solution.py:16
  21.1 104.9 %reduce-scatter.3.cloned.1.call-start = ((), (), s32[]{:S(2)}) async-start(), calls=%async_computation.4 | async-start | bytes 3145728 | tf_op jit(solution)/shard_map/reduce_scatter | solution.py:41
  25.0 1.3 copy-start.19
  47.1 2.9 %copy-start.22 = (s32[1,1,32]{2,1,0:T(1,128)S(1)}, s32[1,1,32]{2,1,0:T(1,128)}, u32[]{:S(2)}) copy-start(s32[1,1,32]{2,1,0:T(1,128)} %param.11) | copy-start | bytes 388
  94.6 2.6 %copy-start.7 = (bf16[8,256,128]{2,1,0:T(8,128)(2,1)S(1)}, bf16[8,256,128]{2,1,0:T(8,128)(2,1)}, u32[]{:S(2)}) copy-start(bf16[8,256,128]{2,1,0:T(8,128)(2,1)} %gather_fusion.3) | copy-start | bytes 1572868
  94.6 2.6 %copy-start.15 = (bf16[1,1,8,256,256]{3,4,2,1,0:T(8,128)(2,1)S(1)}, bf16[1,1,8,256,256]{3,4,2,1,0:T(8,128)(2,1)}, u32[]{:S(2)}) copy-start(bf16[1,1,8,256,256]{3,4,2,1,0:T(8,128)(2,1)} %copy.41) | copy-start | bytes 3145732
  96.4 0.8 copy-start.8
  96.4 2.8 %copy-start.10 = (bf16[1,2048,128]{2,1,0:T(8,128)(2,1)}, bf16[1,2048,128]{2,1,0:T(8,128)(2,1)S(1)}, u32[]{:S(2)}) copy-start(bf16[1,2048,128]{2,1,0:T(8,128)(2,1)S(1)} %get-tuple-element.17) | copy-start | bytes 1572868
  96.4 5.9 %copy-start.12 = (bf16[1,2048,128]{2,1,0:T(8,128)(2,1)}, bf16[1,2048,128]{2,1,0:T(8,128)(2,1)S(1)}, u32[]{:S(2)}) copy-start(bf16[1,2048,128]{2,1,0:T(8,128)(2,1)S(1)} %get-tuple-element.18) | copy-start | bytes 1572868
  96.4 9.0 %copy-start.14 = (bf16[1,2048,128]{2,1,0:T(8,128)(2,1)}, bf16[1,2048,128]{2,1,0:T(8,128)(2,1)S(1)}, u32[]{:S(2)}) copy-start(bf16[1,2048,128]{2,1,0:T(8,128)(2,1)S(1)} %get-tuple-element.16) | copy-start | bytes 1572868
  97.2 2.0 copy-start.6
  97.2 2.0 copy-start.18
  98.7 1.6 copy-start.3
  100.3 2.0 copy-start.5
  100.3 2.0 copy-start.17
  101.7 1.6 copy-start.2
  103.3 2.1 copy-start.4
  103.3 2.1 copy-start.16
  104.9 1.6 copy-start.1
  108.0 1.0 copy-start
  111.2 1.9 copy-start.13
  111.3 2.3 copy-start.11
  113.2 1.0 copy-start.9
  119.6 63.5 %copy-start.21 = (f32[1,128,128]{2,1,0:T(8,128)S(1)}, f32[1,128,128]{2,1,0:T(8,128)}, u32[]{:S(2)}) copy-start(f32[1,128,128]{2,1,0:T(8,128)} %param.8) | copy-start | bytes 196612
  119.7 127.5 %copy-start.20 = (f32[1,256,128]{2,1,0:T(8,128)S(1)}, f32[1,256,128]{2,1,0:T(8,128)}, u32[]{:S(2)}) copy-start(f32[1,256,128]{2,1,0:T(8,128)} %param.7) | copy-start | bytes 393220
  120.7 62.3 %all-to-all-start.1 = ((bf16[16,128,128]{2,1,0:T(8,128)(2,1)}), bf16[16,128,128]{2,1,0:T(8,128)(2,1)S(1)}, u32[]{:S(2)}, u32[]{:S(2)}) async-start(bf16[16,128,128]{2,1,0:T(8,128)(2,1)} %convert_element_type.106), calls=%async_computation.3 | async-start | bytes 1048576 | tf_op jit(solution)/shard_map/all_to_all | solution.py:47
  125.9 121.2 %reduce-scatter.5.cloned.1.call-start = ((), (), s32[]{:S(2)}) async-start(), calls=%async_computation.5 | async-start | bytes 1114112 | tf_op jit(solution)/shard_map/reduce_scatter | solution.py:42
Sparse Core Ops, SparseCore 0:
  11.7 82.8 all-gather.2
  111.3 14.6 reduce-scatter.2
  130.8 116.3 reduce-scatter.4
where the time goes:
time: 257 us; the launch traced here: 256 us
  waiting for transfers between devices  103 us (40%)
  blocking collectives  51.9 us (20%)
  local copies, waits for them, and re-layouts  45 us (18%)
  between operations  19.7 us (8%)
  matrix products  16.1 us (6%)
  starting transfers between devices  14.5 us (6%)
  other arithmetic  6.22 us (2%)
    reduce_scatter x1, waiting for transfers between devices, sum_by_chip(): return lax.psum_scatter(tiles, chips, scatter_dimension=0, tiled=True)[0]  63.4 us
    psum x5, blocking collectives, by_axis(): array = lax.psum(array, axis)  51.9 us
    all_gather x1, waiting for transfers between devices, per_device(): u_band = lax.all_gather(u_low, COLS, axis=0, tiled=True)  38.8 us
    shift_right_arithmetic x11, local copies, waits for them, and re-layouts, decode(): jnp.right_shift(mask_bits[:, :, None, :], shifts[None, None, :, None])  16.8 us
    unnamed x50, local copies, waits for them, and re-layouts  13.2 us
    all_to_all x1, starting transfers between devices, from_everyone(): return lax.all_to_all(copies, axis, split_axis=0, concat_axis=0, tiled=True)  9.17 us
    dot_general x4, matrix products, slot_terms(): jnp.einsum('sik,sjk->sij', left_rows, right_rows, preferred_element_type=...  5.97 us
    gather x4, local copies, waits for them, and re-layouts, slot_terms(): right_rows = jnp.take(right_tiles, column_ids, axis=0)  5.66 us
  transfers between devices with their start and end apart: 5, of which 3 were waited for; matrix products, arithmetic and copies ran while one was open for 18% of the time, Pallas kernels for 0%

commit v1 on v0

--- a/solution.py
+++ b/solution.py
@@ -126,7 +126,9 @@
     v_band = gathered_copies(owned_right.astype(jnp.bfloat16), ROWS, 0)
     right_tiles = v_band.reshape(-1, tile_size, factor_rank)
     u_low = owned_left.astype(jnp.bfloat16)
-    u_band = lax.all_gather(u_low, COLS, axis=0, tiled=True)
+    u_band = jnp.concatenate(
+        lax.all_to_all(jnp.stack([u_low] * lax.axis_size(COLS)), COLS, 0, 0), axis=0
+    )
     first_rows, col_total, square_total = band_terms(
         u_band.reshape(-1, tile_size, factor_rank), tile_values, mask_bits, column_ids, right_tiles
     )

time: 257 us -> 310 us (1.21)
  waiting for transfers between devices: 103 us -> 138 us
  starting transfers between devices: 14.5 us -> 32 us
    all_to_all x0 -> x1, waiting for transfers between devices: none -> 61.9 us  [per_device(): lax.all_to_all(jnp.stack([u_low] * lax.axis_size(COLS)), COLS, 0, 0)]
    all_gather x1 -> x0, waiting for transfers between devices: 38.8 us -> none  [per_device(): u_band = lax.all_gather(u_low, COLS, axis=0, tiled=True)]
    all_to_all x0 -> x1, starting transfers between devices: none -> 15.2 us  [per_device(): lax.all_to_all(jnp.stack([u_low] * lax.axis_size(COLS)), COLS, 0, 0)]
    all_to_all x1, waiting for transfers between devices: 0.01 us -> 12.1 us  [from_everyone(): return lax.all_to_all(copies, axis, split_axis=0, concat_axis=0, tiled=True)]
    unnamed x50 -> x42, local copies, waits for them, and re-layouts: 13.2 us -> 13 us
  transfers between devices with their start and end apart: 5 -> 5, of which waited for: 3 -> 3; matrix products, arithmetic and copies ran while one was open for 18% -> 16% of each run, Pallas kernels for 0% -> 0%
where the time goes in v1:
time: 310 us; the launch traced here: 309 us
  waiting for transfers between devices  138 us (45%)
  blocking collectives  49.5 us (16%)
  local copies, waits for them, and re-layouts  46.1 us (15%)
  starting transfers between devices  32 us (10%)
  between operations  19.9 us (6%)
  matrix products  18.2 us (6%)
  other arithmetic  5.62 us (2%)
    reduce_scatter x1, waiting for transfers between devices, sum_by_chip(): return lax.psum_scatter(tiles, chips, scatter_dimension=0, tiled=True)[0]  63.4 us
    all_to_all x1, waiting for transfers between devices, per_device(): lax.all_to_all(jnp.stack([u_low] * lax.axis_size(COLS)), COLS, 0, 0)  61.9 us
    psum x5, blocking collectives, by_axis(): array = lax.psum(array, axis)  49.5 us
    shift_right_arithmetic x11, local copies, waits for them, and re-layouts, decode(): jnp.right_shift(mask_bits[:, :, None, :], shifts[None, None, :, None])  17.8 us
    all_to_all x1, starting transfers between devices, per_device(): lax.all_to_all(jnp.stack([u_low] * lax.axis_size(COLS)), COLS, 0, 0)  15.2 us
    unnamed x42, local copies, waits for them, and re-layouts  13 us
    all_to_all x1, waiting for transfers between devices, from_everyone(): return lax.all_to_all(copies, axis, split_axis=0, concat_axis=0, tiled=True)  12.1 us
    all_to_all x1, starting transfers between devices, from_everyone(): return lax.all_to_all(copies, axis, split_axis=0, concat_axis=0, tiled=True)  9.17 us
  transfers between devices with their start and end apart: 5, of which 3 were waited for; matrix products, arithmetic and copies ran while one was open for 16% of the time, Pallas kernels for 0%

profile of v1, /device:TPU:8, one launch (start us, length us, event | category | flops | bytes accessed | tf_op | source)
XLA Modules:
  0.0 309.4 jit_solution(4806306272726124063)
XLA Ops:
  7.2 1.5 multiply_reduce_fusion.5
  8.7 0.9 broadcast_in_dim.11
  9.6 9.2 %all-to-all-start = ((bf16[16,128,128]{2,1,0:T(8,128)(2,1)}), bf16[16,128,128]{2,1,0:T(8,128)(2,1)S(1)}, u32[]{:S(2)}, u32[]{:S(2)}) async-start(bf16[16,128,128]{2,1,0:T(8,128)(2,1)} %broadcast_in_dim.11), calls=%async_computation | async-start | bytes 1048576 | tf_op jit(solution)/shard_map/all_to_all | solution.py:16
  18.8 1.6 multiply_reduce_fusion.4
  20.4 12.1 %all-to-all-done = bf16[16,128,128]{2,1,0:T(8,128)(2,1)S(1)} async-done(((bf16[16,128,128]{2,1,0:T(8,128)(2,1)}), bf16[16,128,128]{2,1,0:T(8,128)(2,1)S(1)}, u32[]{:S(2)}, u32[]{:S(2)}) %all-to-all-start) | async-done | bytes 524320 | tf_op jit(solution)/shard_map/all_to_all | solution.py:16
  32.5 1.8 stack.5
  34.3 15.2 %all-to-all-start.1 = ((bf16[32,256,128]{2,1,0:T(8,128)(2,1)}), bf16[32,256,128]{2,1,0:T(8,128)(2,1)S(1)}, u32[]{:S(2)}, u32[]{:S(2)}) async-start(bf16[32,256,128]{2,1,0:T(8,128)(2,1)} %stack.5), calls=%async_computation.1 | async-start | bytes 4194304 | tf_op jit(solution)/shard_map/all_to_all | solution.py:130
  49.6 4.3 %fusion.44 = (bf16[1,1,8,256,256]{4,3,2,1,0:T(8,128)(2,1)}, bf16[1,1,8,256,256]{4,3,2,1,0:T(8,128)(2,1)}, bf16[1,1,8,256,256]{4,3,2,1,0:T(8,128)(2,1)}, bf16[1,1,8,256,256]{4,3,2,1,0:T(8,128)(2,1)}) fusion(bf16[1,1,32,256,256]{4,3,2,1,0:T(8,128)(2,1)} %param.9), kind=kLoop, calls=%fused_computation.103 | loop fusion | bytes 8388608 | tf_op jit(solution)/shard_map/slice | solution.py:106
  53.9 2.4 copy.41
  56.3 1.5 shift_right_arithmetic.104
  57.8 2.9 copy.30
  60.7 0.1 shift_right_arithmetic.92
  60.7 2.3 copy.40
  63.0 1.5 shift_right_arithmetic.100
  64.5 2.9 copy.27
  67.4 2.3 copy.39
  69.7 1.5 shift_right_arithmetic.96
  71.2 2.9 copy.24
  74.1 2.3 copy.38
  76.4 1.5 shift_right_arithmetic.89
  77.9 2.9 copy.21
  80.8 0.1 compare_and_fusion.3
  80.9 1.4 gather_fusion.3
  82.4 1.4 gather_fusion.2
  83.8 1.4 gather_fusion.1
  85.2 1.4 gather_fusion
  86.6 61.9 %all-to-all-done.1 = bf16[32,256,128]{2,1,0:T(8,128)(2,1)S(1)} async-done(((bf16[32,256,128]{2,1,0:T(8,128)(2,1)}), bf16[32,256,128]{2,1,0:T(8,128)(2,1)S(1)}, u32[]{:S(2)}, u32[]{:S(2)}) %all-to-all-start.1) | async-done | bytes 2097184 | tf_op jit(solution)/shard_map/all_to_all | solution.py:130
  148.5 3.6 %multiply_reduce_fusion = (f32[]{:T(128)}, bf16[8,256,256]{1,2,0:T(8,128)(2,1)S(1)}) fusion(bf16[1,1,8,256,256]{3,4,2,1,0:T(8,128)(2,1)} %copy.41, bf16[32,256,128]{2,1,0:T(8,128)(2,1)S(1)} %all-to-all-done.1, bf16[8,256,128]{2,1,0:T(8,128)(2,1)} %gather_fusion.3, pred[8]{0:T(512)(128)(4,1)S(1)} %get-tuple-element.28, s32[8,256,256]{1,2,0:T(8,128)} %copy.30, ...), kind=kOutput, calls=%fused_computation.17 | convolution fusion | flops 139198464 | bytes 5244420 | tf_op jit(solution)/shard_map/sik,sjk->sij/dot_general | solution.py:70
  152.2 0.5 convolution_convert_fusion
  152.7 0.5 copy-done.7
  153.2 0.3 copy-done.14
  153.5 1.5 multiply_reduce_fusion.1
  155.0 0.5 convolution_convert_fusion.1
  155.6 0.9 copy-done.6
  156.4 0.4 copy-done.13
  156.8 1.5 multiply_reduce_fusion.2
  158.3 0.5 convolution_convert_fusion.2
  158.9 0.9 copy-done.5
  159.8 0.4 copy-done.12
  160.1 1.5 multiply_reduce_fusion.3
  161.6 0.5 convolution_convert_fusion.3
  162.1 0.5 copy-done.4
  162.6 0.1 pad_maximum_fusion
  162.7 1.6 copy.33
  164.4 1.8 convolution_bitcast_fusion.3
  166.2 0.4 convolution_bitcast_fusion.2
  166.7 0.4 convolution_bitcast_fusion.1
  167.1 0.4 convolution_bitcast_fusion
  167.5 1.2 fusion.11
  168.8 1.2 convolution_add_fusion.2
  170.0 1.2 convolution_add_fusion.1
  171.2 1.3 fusion
  172.5 1.0 convert_element_type.103
  173.6 7.5 %all-to-all-start.2 = ((bf16[16,128,128]{2,1,0:T(8,128)(2,1)}), bf16[16,128,128]{2,1,0:T(8,128)(2,1)S(1)}, u32[]{:S(2)}, u32[]{:S(2)}) async-start(bf16[16,128,128]{2,1,0:T(8,128)(2,1)} %convert_element_type.103), calls=%async_computation.4 | async-start | bytes 1048576 | tf_op jit(solution)/shard_map/all_to_all | solution.py:47
  181.1 0.7 reduce-scatter.5.cloned.1.call-update
  185.7 9.1 %psum.35 = f32[]{:T(128)} all-reduce(f32[]{:T(128)S(6)} %add.61), channel_id=1, replica_groups=mesh['rows_0'=4,'rows_1'=4,'cols_0'=4,'cols_1'=4,'cols_2'=2] {'rows_0'}, use_global_device_ids=true, to_apply=%region_9.11 | all-reduce | flops 1 | bytes 8 | tf_op jit(solution)/shard_map/psum | solution.py:53
  194.8 12.2 %psum.36 = f32[]{:T(128)} all-reduce(f32[]{:T(128)} %psum.35), channel_id=1, replica_groups=mesh['rows_0'=4,'rows_1'=4,'cols_0'=4,'cols_1'=4,'cols_2'=2] {'rows_1'}, use_global_device_ids=true, to_apply=%region_10.12 | all-reduce | flops 1 | bytes 8 | tf_op jit(solution)/shard_map/psum | solution.py:53
  207.0 14.2 %psum.37 = f32[]{:T(128)} all-reduce(f32[]{:T(128)} %psum.36), channel_id=1, replica_groups=mesh['rows_0'=4,'rows_1'=4,'cols_0'=4,'cols_1'=4,'cols_2'=2] {'cols_0'}, use_global_device_ids=true, to_apply=%region_11.13 | all-reduce | flops 1 | bytes 8 | tf_op jit(solution)/shard_map/psum | solution.py:53
  221.3 10.8 %psum.38 = f32[]{:T(128)} all-reduce(f32[]{:T(128)} %psum.37), channel_id=1, replica_groups=mesh['rows_0'=4,'rows_1'=4,'cols_0'=4,'cols_1'=4,'cols_2'=2] {'cols_1'}, use_global_device_ids=true, to_apply=%region_12.14 | all-reduce | flops 1 | bytes 8 | tf_op jit(solution)/shard_map/psum | solution.py:53
  232.1 3.1 psum.39
  235.8 0.1 convert_reduce_fusion
  235.9 0.6 fusion.31
  236.5 63.4 %reduce-scatter.5.cloned.1.call-done = bf16[1,256,128]{2,1,0:T(8,128)(2,1)} async-done(((bf16[16,256,128]{2,1,0:T(8,128)(2,1)}), bf16[1,256,128]{2,1,0:T(8,128)(2,1)}) %reduce-scatter.5.cloned.1.call-update) | async-done | bytes 65552 | tf_op jit(solution)/shard_map/reduce_scatter | solution.py:42
  299.9 1.5 multiply_subtract_fusion
  (41 shorter events, 0.3 us)
Async XLA Ops:
  9.6 22.9 %all-to-all-start = ((bf16[16,128,128]{2,1,0:T(8,128)(2,1)}), bf16[16,128,128]{2,1,0:T(8,128)(2,1)S(1)}, u32[]{:S(2)}, u32[]{:S(2)}) async-start(bf16[16,128,128]{2,1,0:T(8,128)(2,1)} %broadcast_in_dim.11), calls=%async_computation | async-start | bytes 1048576 | tf_op jit(solution)/shard_map/all_to_all | solution.py:16
  34.3 114.2 %all-to-all-start.1 = ((bf16[32,256,128]{2,1,0:T(8,128)(2,1)}), bf16[32,256,128]{2,1,0:T(8,128)(2,1)S(1)}, u32[]{:S(2)}, u32[]{:S(2)}) async-start(bf16[32,256,128]{2,1,0:T(8,128)(2,1)} %stack.5), calls=%async_computation.1 | async-start | bytes 4194304 | tf_op jit(solution)/shard_map/all_to_all | solution.py:130
  49.6 131.6 %reduce-scatter.3.cloned.1.call-start = ((), (), s32[]{:S(2)}) async-start(), calls=%async_computation.5 | async-start | bytes 3145728 | tf_op jit(solution)/shard_map/reduce_scatter | solution.py:41
  53.9 2.4 copy-start.15
  77.9 3.0 copy-start.18
  148.5 3.7 %copy-start.8 = (bf16[8,256,128]{2,1,0:T(8,128)(2,1)S(1)}, bf16[8,256,128]{2,1,0:T(8,128)(2,1)}, u32[]{:S(2)}) copy-start(bf16[8,256,128]{2,1,0:T(8,128)(2,1)} %gather_fusion.3) | copy-start | bytes 1572868
  148.5 4.2 %copy-start.11 = (s32[8,256,256]{1,2,0:T(8,128)S(1)}, s32[8,256,256]{1,2,0:T(8,128)}, u32[]{:S(2)}) copy-start(s32[8,256,256]{1,2,0:T(8,128)} %copy.27) | copy-start | bytes 6291460
  152.2 1.0 copy-start.7
  152.2 1.4 copy-start.14
  153.5 2.0 copy-start.10
  155.0 3.3 %copy-start = (bf16[8,256,256]{1,2,0:T(8,128)(2,1)}, bf16[8,256,256]{1,2,0:T(8,128)(2,1)S(1)}, u32[]{:S(2)}) copy-start(bf16[8,256,256]{1,2,0:T(8,128)(2,1)S(1)} %get-tuple-element.39) | copy-start | bytes 3145732
  155.0 1.4 copy-start.6
  155.0 1.8 copy-start.13
  156.8 2.1 copy-start.9
  158.3 3.3 %copy-start.2 = (bf16[8,256,256]{1,2,0:T(8,128)(2,1)}, bf16[8,256,256]{1,2,0:T(8,128)(2,1)S(1)}, u32[]{:S(2)}) copy-start(bf16[8,256,256]{1,2,0:T(8,128)(2,1)S(1)} %get-tuple-element.37) | copy-start | bytes 3145732
  158.3 1.4 copy-start.5
  158.3 1.8 copy-start.12
  161.6 1.0 copy-start.4
  164.3 1.9 copy-start.3
  164.4 2.2 copy-start.1
  172.5 63.4 %copy-start.17 = (f32[1,128,128]{2,1,0:T(8,128)S(1)}, f32[1,128,128]{2,1,0:T(8,128)}, u32[]{:S(2)}) copy-start(f32[1,128,128]{2,1,0:T(8,128)} %param.8) | copy-start | bytes 196612
  172.5 127.4 %copy-start.16 = (f32[1,256,128]{2,1,0:T(8,128)S(1)}, f32[1,256,128]{2,1,0:T(8,128)}, u32[]{:S(2)}) copy-start(f32[1,256,128]{2,1,0:T(8,128)} %param.7) | copy-start | bytes 393220
  173.6 62.2 %all-to-all-start.2 = ((bf16[16,128,128]{2,1,0:T(8,128)(2,1)}), bf16[16,128,128]{2,1,0:T(8,128)(2,1)S(1)}, u32[]{:S(2)}, u32[]{:S(2)}) async-start(bf16[16,128,128]{2,1,0:T(8,128)(2,1)} %convert_element_type.103), calls=%async_computation.4 | async-start | bytes 1048576 | tf_op jit(solution)/shard_map/all_to_all | solution.py:47
  181.1 118.8 %reduce-scatter.5.cloned.1.call-start = ((), (), s32[]{:S(2)}) async-start(), calls=%async_computation.6 | async-start | bytes 1114112 | tf_op jit(solution)/shard_map/reduce_scatter | solution.py:42
Sparse Core Ops, SparseCore 0:
  164.5 14.2 reduce-scatter.2
  186.0 113.9 reduce-scatter.4
